TPU v7x, 256 devices: a 4x2x16 block of a 4x16x16 slice. The times are simulated.
256 devices in a mesh: parts: 2 (over y), dp: 64 (over x, z), tensor: 2 (over core).
Axes of the slice: x: 4, y: 2, z: 16, core: 2. Of those that a mesh axis runs over, the one named last changes fastest.
The devices are a block of a 4x16x16 slice.
Arguments:
- normed: bfloat16 [128, 256, 4096], P(('parts', 'dp')), parts along dimension 0, may hold values from -28 to 28
- q_weight: bfloat16 [4096, 2048], P('dp', 'tensor'), may hold values from -0.09375 to 0.09375
- kv_weight: bfloat16 [4096, 2, 512], P('dp', None, 'tensor'), may hold values from -0.09375 to 0.09375
- o_weight: bfloat16 [2048, 4096], P('tensor', 'dp'), may hold values from -0.5 to 0.5
- lengths: int32 [128], P(('parts', 'dp')), parts along dimension 0, may hold values from 64 to 256
- destinations: int32 [128], P(('parts', 'dp')), parts along dimension 0, may hold values from 0 to 63, each once
Outputs:
- projected: bfloat16 [128, 256, 4096], P(('parts', 'dp'), None, 'tensor'), parts along dimension 0
- kv_cache: bfloat16 [128, 2, 4, 256, 128], P(('parts', 'dp'), None, None, 'tensor'), parts along dimension 0
There are 2 independent parts, one for each index of `parts`. A program takes and returns all parts, laid end to end along the dimension named above; an argument that names none is the same for every part. Nothing has to cross between parts.
All inputs are finite; a program needn't handle non-finite values.
Results may differ from a plain program's by a relative error of at most 0.012.
The roundings to bfloat16 on the way count: a program that leaves them out, or rounds other values in their place, can miss the bound.
Values may be sent and summed in bfloat16 or wider, within the bound.
No kernel may reach another device: no remote copies, remote signals or barrier semaphores. Data moves between devices by JAX's collectives and lax.ppermute only.
A program may use at most 128 MiB of HBM per device.

v0:
```python
import math
import jax
import jax.numpy as jnp
from jax import lax
from jax.sharding import PartitionSpec as P

HD = 128
ROPE_BASE = 500000.0


def copy_for_each(array, axis):
    copies = jnp.broadcast_to(array, (lax.axis_size(axis), *array.shape))
    return lax.all_to_all(copies, axis, split_axis=0, concat_axis=0, tiled=True)


def in_order(blocks, dim):
    blocks = jnp.moveaxis(blocks, 0, dim)
    lengths = blocks.shape
    return blocks.reshape(*lengths[:dim], lengths[dim] * lengths[dim + 1], *lengths[dim + 2 :])


def gather_directly(array, axis, dim):
    blocks = copy_for_each(array, axis)
    return in_order(blocks, dim)


def in_one_piece(arrays, axis, dim, along):
    widths = [math.prod(a.shape[along:]) for a in arrays]
    both = jnp.concatenate(
        [a.reshape(*a.shape[:along], w) for a, w in zip(arrays, widths)], axis=along
    )
    filled = lax.all_gather(both, axis, axis=dim, tiled=True)
    blocks = jnp.split(filled, [sum(widths[:k]) for k in range(1, len(widths))], axis=along)
    return tuple(
        (b.reshape(*filled.shape[:along], *a.shape[along:]) for a, b in zip(arrays, blocks))
    )


def in_blocks(array, dim, size):
    before, after = (array.shape[:dim], array.shape[dim + 1 :])
    return jnp.moveaxis(array.reshape(*before, size, -1, *after), dim, 0)


def summed_on_arrival(array, axis, dim):
    size = lax.axis_size(axis)
    blocks = lax.all_to_all(in_blocks(array, dim, size), axis, 0, 0, tiled=True)
    return jnp.sum(blocks, axis=0)


def rotate(values, positions):
    half = values.shape[-1] // 2
    steps = jnp.arange(half, dtype=jnp.float32) * (2.0 / values.shape[-1])
    freq = jnp.power(jnp.float32(ROPE_BASE), -steps)
    angle = positions.astype(jnp.float32)[:, None] * freq[None, :]
    cosine = jnp.cos(angle)[:, None, :]
    sine = jnp.sin(angle)[:, None, :]
    first = values[..., :half]
    second = values[..., half:]
    return jnp.concatenate(
        [first * cosine - second * sine, second * cosine + first * sine], axis=-1
    )


def attend(queries, keys, values, length):
    total = keys.shape[1]
    block = min(total, 512)
    count = total // block
    key_pos = jnp.arange(total, dtype=jnp.int32)

    def one_block(index):
        start = index * block
        scores = jnp.einsum(
            "kgqd,ktd->kgqt", queries, keys, preferred_element_type=jnp.float32
        ) / math.sqrt(HD)
        query_pos = start + jnp.arange(block, dtype=jnp.int32)
        allowed = (query_pos[:, None] >= key_pos[None, :]) & (key_pos[None, :] < length)
        scores = jnp.where(allowed, scores, -jnp.inf)
        peak = jnp.max(scores, axis=-1, keepdims=True)
        expo = jnp.exp(scores - peak)
        weights = (expo / jnp.sum(expo, axis=-1, keepdims=True)).astype(jnp.bfloat16)
        return jnp.einsum(
            "kgqt,ktd->kgqd", weights, values, preferred_element_type=jnp.float32
        ).astype(jnp.bfloat16)

    blocks = lax.map(one_block, jnp.arange(count, dtype=jnp.int32))
    return blocks.transpose(0, 3, 1, 2, 4).reshape(total, -1)


def regroup(cache):
    return lax.all_to_all(cache, "tensor", split_axis=2, concat_axis=1, tiled=True)


def deliver(cache, destination):
    count = lax.axis_size("dp")
    flat = cache.reshape(count, -1)
    sent_to = gather_directly(destination, "dp", 0)
    spread = lax.all_to_all(flat, "dp", split_axis=0, concat_axis=0, tiled=True)
    slots = jnp.arange(count, dtype=jnp.int32)
    match = sent_to[None, :] == slots[:, None]
    source = jnp.sum(jnp.where(match, slots[None, :], 0), axis=1)
    outgoing = jnp.take(spread, source, axis=0)
    arrived = lax.all_to_all(outgoing, "dp", split_axis=0, concat_axis=0, tiled=True)
    return arrived.reshape(cache.shape)


def on_device(normed, q_weight, kv_weight, o_weight, lengths, destinations):
    tokens = normed[0]
    total = tokens.shape[0]
    q_local = q_weight.shape[1] // HD
    kv_local = kv_weight.shape[2] // HD
    group = q_local // kv_local
    q_full, kv_full = in_one_piece((q_weight, kv_weight), "dp", 0, 1)
    query_raw = jnp.dot(tokens, q_full, preferred_element_type=jnp.float32)
    pair_raw = jnp.dot(
        tokens, kv_full.reshape(kv_full.shape[0], -1), preferred_element_type=jnp.float32
    )
    positions = jnp.arange(total, dtype=jnp.int32)
    query = rotate(query_raw.reshape(total, q_local, HD), positions).astype(jnp.bfloat16)
    pair = pair_raw.reshape(total, 2, kv_local, HD)
    keys = rotate(pair[:, 0], positions).astype(jnp.bfloat16)
    values = pair[:, 1].astype(jnp.bfloat16)
    grouped = query.reshape(total, kv_local, group, HD).transpose(1, 2, 0, 3)
    key_rows = keys.transpose(1, 0, 2)
    value_rows = values.transpose(1, 0, 2)
    length = lengths[0]
    attended = attend(grouped, key_rows, value_rows, length)
    partial_sums = jnp.dot(
        attended,
        lax.all_gather(o_weight, "dp", axis=1, tiled=True),
        preferred_element_type=jnp.float32,
    )
    projected = summed_on_arrival(partial_sums, "tensor", 1).astype(jnp.bfloat16)
    live = (positions < length)[None, :, None]
    kept_keys = jnp.where(live, key_rows, jnp.zeros_like(key_rows))
    kept_values = jnp.where(live, value_rows, jnp.zeros_like(value_rows))
    cache = jnp.stack([kept_keys, kept_values], axis=0)
    routed = deliver(regroup(cache), destinations)
    return (projected[None], routed[None])


def solution(mesh):
    placed = (
        P(("parts", "dp"), None, None),
        P("dp", "tensor"),
        P("dp", None, "tensor"),
        P("tensor", "dp"),
        P(("parts", "dp")),
        P(("parts", "dp")),
    )
    return jax.shard_map(
        on_device,
        mesh=mesh,
        in_specs=placed,
        out_specs=(
            P(("parts", "dp"), None, "tensor"),
            P(("parts", "dp"), None, None, "tensor", None),
        ),
        check_vma=False,
    )
```

profile of v0, /device:TPU:38, one launch (start us, length us, event | category | flops | bytes accessed | tf_op | source)
XLA Modules:
  0.0 402.5 jit_solution(113619744113657147)
XLA Ops:
  7.3 1.0 copy.79
  8.2 1.6 pad_maximum_fusion.1
  9.9 0.1 all-gather.5.cloned.1.call-start
  10.0 0.7 all-gather.5.cloned.1.call-update
  11.4 0.6 broadcast_in_dim.76
  12.0 28.4 %all-to-all-start.1 = ((s32[64,1,1]{2,1,0:T(1,128)}), s32[64,1,1]{2,1,0:T(1,128)S(1)}, u32[]{:S(2)}, u32[]{:S(2)}) async-start(s32[64,1,1]{2,1,0:T(1,128)} %broadcast_in_dim.76), calls=%async_computation.1 | async-start | bytes 65536 | tf_op jit(solution)/shard_map/all_to_all | solution.py:13
  41.1 0.3 multiply_cosine_fusion
  41.4 0.7 fusion.14
  42.1 0.7 copy.60
  42.8 0.7 copy.59
  43.6 8.7 %all-to-all-done.1 = s32[64,1,1]{2,1,0:T(1,128)S(1)} async-done(((s32[64,1,1]{2,1,0:T(1,128)}), s32[64,1,1]{2,1,0:T(1,128)S(1)}, u32[]{:S(2)}, u32[]{:S(2)}) %all-to-all-start.1) | async-done | bytes 288 | tf_op jit(solution)/shard_map/all_to_all | solution.py:13
  52.2 1.2 reduce
  53.5 0.1 select_reduce_fusion
  53.6 135.9 %all-gather.3.cloned.1.call-done = bf16[4096,1536]{1,0:T(8,128)(2,1)} async-done(((bf16[64,1536]{1,0:T(8,128)(2,1)}), bf16[4096,1536]{1,0:T(8,128)(2,1)}) %all-gather.3.cloned.1.call-update) | async-done | bytes 12582928 | tf_op jit(solution)/shard_map/all_gather | solution.py:32
  189.5 3.5 fusion.3
  193.0 5.8 %fusion.1 = f32[1024,256]{1,0:T(8,128)S(1)} fusion(bf16[4096,1536]{1,0:T(8,128)(2,1)} %all-gather.3.cloned.1.call-done, bf16[1,256,4096]{2,1,0:T(8,128)(2,1)S(1)} %copy-done), kind=kOutput, calls=%fused_computation.2 | convolution fusion | flops 2147483648 | bytes 11534336 | tf_op jit(solution)/shard_map/dot_general | solution.py:113
  198.8 0.2 subtract_convert_fusion
  199.0 0.3 copy.57
  199.3 1.0 copy.56
  200.3 0.1 copy.77
  200.4 0.1 copy.78
  200.5 1.2 subtract_convert_fusion.1
  201.7 0.1 fusion.22
  201.9 0.3 copy.65
  202.2 4.0 all_to_all.45
  206.2 0.1 all_to_all.39
  206.3 0.5 broadcast.133
  206.9 2.1 reduce.2
  209.0 0.9 reshape.172
  209.9 12.5 %all-to-all-start.3 = ((bf16[64,2,1024]{2,1,0:T(2,128)(2,1)}), bf16[64,2,1024]{2,1,0:T(2,128)(2,1)S(1)}, u32[]{:S(2)}, u32[]{:S(2)}) async-start(bf16[64,2,1024]{2,1,0:T(2,128)(2,1)} %reshape.172), calls=%async_computation.3 | async-start | bytes 524288 | tf_op jit(solution)/shard_map/all_to_all | solution.py:97
  222.4 3.5 fusion.30
  225.9 1.9 convolution_convert_fusion
  227.8 114.4 %all-gather.5.cloned.1.call-done = bf16[1024,4096]{0,1:T(8,128)(2,1)} async-done(((bf16[1024,64]{0,1:T(8,128)(2,1)}), bf16[1024,4096]{0,1:T(8,128)(2,1)}) %all-gather.5.cloned.1.call-update) | async-done | bytes 8388624 | tf_op jit(solution)/shard_map/all_gather | solution.py:129
  342.3 7.7 %convolution_bitcast_fusion = f32[2,256,2048]{2,1,0:T(8,128)} fusion(bf16[256,1024,1]{0,1,2:T(8,128)(2,1)S(1)} %bitcast.109, bf16[2,2048,1024]{2,1,0:T(8,128)(2,1)} %bitcast.108), kind=kOutput, calls=%fused_computation.6 | convolution fusion | flops 2147483648 | bytes 13107200 | tf_op jit(solution)/shard_map/dot_general | solution.py:127
  350.0 5.6 %all-to-all-start = ((f32[2,256,2048]{2,1,0:T(8,128)}), f32[2,256,2048]{2,1,0:T(8,128)}, u32[]{:S(2)}, u32[]{:S(2)}) async-start(f32[2,256,2048]{2,1,0:T(8,128)} %convolution_bitcast_fusion), calls=%async_computation | async-start | bytes 8388608 | tf_op jit(solution)/shard_map/all_to_all | solution.py:46
  355.6 0.2 reshape.173
  355.9 0.2 copy.82
  356.0 0.7 gather_fusion
  356.8 0.1 bitcast_select_fusion
  356.9 0.7 reduce.3
  357.6 0.9 reshape.174
  358.5 1.6 all-to-all-done
  360.1 12.5 %all-to-all-start.4 = ((bf16[64,2,1024]{2,1,0:T(2,128)(2,1)}), bf16[64,2,1024]{2,1,0:T(2,128)(2,1)S(1)}, u32[]{:S(2)}, u32[]{:S(2)}) async-start(bf16[64,2,1024]{2,1,0:T(2,128)(2,1)} %reshape.174), calls=%async_computation.4 | async-start | bytes 524288 | tf_op jit(solution)/shard_map/all_to_all | solution.py:102
  372.6 3.8 reduce_sum.31
  376.3 16.7 %all-to-all-done.4 = bf16[64,2,1024]{2,1,0:T(2,128)(2,1)S(1)} async-done(((bf16[64,2,1024]{2,1,0:T(2,128)(2,1)}), bf16[64,2,1024]{2,1,0:T(2,128)(2,1)S(1)}, u32[]{:S(2)}, u32[]{:S(2)}) %all-to-all-start.4) | async-done | bytes 262176 | tf_op jit(solution)/shard_map/all_to_all | solution.py:102
  393.1 0.2 reshape.175
  393.3 1.5 reduce.1
  394.8 0.8 broadcast_in_dim_reshape.4
  (21 shorter events, 0.3 us)
Async XLA Ops:
  7.2 182.3 %copy-start = (bf16[1,256,4096]{2,1,0:T(8,128)(2,1)S(1)}, bf16[1,256,4096]{2,1,0:T(8,128)(2,1)}, u32[]{:S(2)}) copy-start(bf16[1,256,4096]{2,1,0:T(8,128)(2,1)} %param.6) | copy-start | bytes 6291460
  7.2 182.3 %all-gather.3.cloned.1.call-start = ((), (), s32[]{:S(2)}) async-start(), calls=%async_computation.5 | async-start | bytes 12779520 | tf_op jit(solution)/shard_map/all_gather | solution.py:32
  9.9 332.4 %all-gather.5.cloned.1.call-start = ((), (), s32[]{:S(2)}) async-start(), calls=%async_computation.6 | async-start | bytes 8519680 | tf_op jit(solution)/shard_map/all_gather | solution.py:129
  12.0 40.2 %all-to-all-start.1 = ((s32[64,1,1]{2,1,0:T(1,128)}), s32[64,1,1]{2,1,0:T(1,128)S(1)}, u32[]{:S(2)}, u32[]{:S(2)}) async-start(s32[64,1,1]{2,1,0:T(1,128)} %broadcast_in_dim.76), calls=%async_computation.1 | async-start | bytes 65536 | tf_op jit(solution)/shard_map/all_to_all | solution.py:13
  200.5 1.4 copy-start.1
  201.7 4.4 %copy-start.3 = (bf16[256,2,64]{2,0,1:T(8,128)(2,1)}, bf16[256,2,64]{2,0,1:T(8,128)(2,1)S(1)}, u32[]{:S(2)}) copy-start(bf16[256,2,64]{2,0,1:T(8,128)(2,1)S(1)} %get-tuple-element.19) | copy-start | bytes 196612
  209.9 140.1 %all-to-all-start.3 = ((bf16[64,2,1024]{2,1,0:T(2,128)(2,1)}), bf16[64,2,1024]{2,1,0:T(2,128)(2,1)S(1)}, u32[]{:S(2)}, u32[]{:S(2)}) async-start(bf16[64,2,1024]{2,1,0:T(2,128)(2,1)} %reshape.172), calls=%async_computation.3 | async-start | bytes 524288 | tf_op jit(solution)/shard_map/all_to_all | solution.py:97
  222.4 3.5 copy-start.2
  350.0 10.1 %all-to-all-start = ((f32[2,256,2048]{2,1,0:T(8,128)}), f32[2,256,2048]{2,1,0:T(8,128)}, u32[]{:S(2)}, u32[]{:S(2)}) async-start(f32[2,256,2048]{2,1,0:T(8,128)} %convolution_bitcast_fusion), calls=%async_computation | async-start | bytes 8388608 | tf_op jit(solution)/shard_map/all_to_all | solution.py:46
  360.1 33.0 %all-to-all-start.4 = ((bf16[64,2,1024]{2,1,0:T(2,128)(2,1)}), bf16[64,2,1024]{2,1,0:T(2,128)(2,1)S(1)}, u32[]{:S(2)}, u32[]{:S(2)}) async-start(bf16[64,2,1024]{2,1,0:T(2,128)(2,1)} %reshape.174), calls=%async_computation.4 | async-start | bytes 524288 | tf_op jit(solution)/shard_map/all_to_all | solution.py:102
Sparse Core Ops, SparseCore 0:
  11.0 178.4 all-gather.2
  191.9 150.3 all-gather.4
where the time goes:
time: 403 us; the launch traced here: 402 us
  waiting for transfers between devices  278 us (69%)
  starting transfers between devices  59.1 us (15%)
  matrix products  22.4 us (6%)
  between operations  15.6 us (4%)
  other arithmetic  13.7 us (3%)
  local copies, waits for them, and re-layouts  9.62 us (2%)
    all_gather x1, waiting for transfers between devices, in_one_piece(): filled = lax.all_gather(both, axis, axis=dim, tiled=True)  136 us
    all_gather x1, waiting for transfers between devices, on_device(): lax.all_gather(o_weight, 'dp', axis=1, tiled=True)  114 us
    all_to_all x1, starting transfers between devices, copy_for_each(): return lax.all_to_all(copies, axis, split_axis=0, concat_axis=0, tiled=True)  28.4 us
    all_to_all x1, waiting for transfers between devices, deliver(): lax.all_to_all(outgoing, 'dp', split_axis=0, concat_axis=0, tiled=True)  16.7 us
    all_to_all x1, starting transfers between devices, deliver(): lax.all_to_all(outgoing, 'dp', split_axis=0, concat_axis=0, tiled=True)  12.5 us
    all_to_all x1, starting transfers between devices, deliver(): spread = lax.all_to_all(flat, 'dp', split_axis=0, concat_axis=0, tiled=True)  12.5 us
    all_to_all x1, waiting for transfers between devices, copy_for_each(): return lax.all_to_all(copies, axis, split_axis=0, concat_axis=0, tiled=True)  8.67 us
  transfers between devices with their start and end apart: 6, of which 5 were waited for; matrix products, arithmetic and copies ran while one was open for 10% of the time, Pallas kernels for 0%

commit v1 on v0

--- a/solution.py
+++ b/solution.py
@@ -126,7 +126,9 @@
     attended = attend(grouped, key_rows, value_rows, length)
     partial_sums = jnp.dot(
         attended,
-        lax.all_gather(o_weight, "dp", axis=1, tiled=True),
+        jnp.concatenate(
+            lax.all_to_all(jnp.stack([o_weight] * lax.axis_size("dp")), "dp", 0, 0), axis=1
+        ),
         preferred_element_type=jnp.float32,
     )
     projected = summed_on_arrival(partial_sums, "tensor", 1).astype(jnp.bfloat16)

time: 403 us -> 684 us (1.70)
  waiting for transfers between devices: 278 us -> 551 us
  blocking collectives: 3.96 us -> 38.8 us
  starting transfers between devices: 59.1 us -> 28.5 us
    all_to_all x2 -> x1, waiting for transfers between devices: 18.3 us -> 346 us  [on_device(): lax.all_to_all(jnp.stack([o_weight] * lax.axis_size('dp')), 'dp', 0, 0)]
    all_gather x1 -> x0, waiting for transfers between devices: 114 us -> none  [on_device(): lax.all_gather(o_weight, 'dp', axis=1, tiled=True)]
    all_gather x1, waiting for transfers between devices: 136 us -> 178 us  [in_one_piece(): filled = lax.all_gather(both, axis, axis=dim, tiled=True)]
    all_to_all x0 -> x2, blocking collectives: none -> 34.9 us  [the longest x1 26.7 us: deliver(): lax.all_to_all(outgoing, 'dp', split_axis=0, concat_axis=0, tiled=True)]
    all_to_all x1, waiting for transfers between devices: 0.01 us -> 18.6 us  [deliver(): spread = lax.all_to_all(flat, 'dp', split_axis=0, concat_axis=0, tiled=True)]
    all_to_all x1, starting transfers between devices: 28.4 us -> 12.5 us  [copy_for_each(): return lax.all_to_all(copies, axis, split_axis=0, concat_axis=0, tiled=True)]
    all_to_all x2 -> x1, starting transfers between devices: 18.1 us -> 7.9 us  [on_device(): lax.all_to_all(jnp.stack([o_weight] * lax.axis_size('dp')), 'dp', 0, 0)]
  transfers between devices with their start and end apart: 6 -> 4, of which waited for: 5 -> 4; matrix products, arithmetic and copies ran while one was open for 10% -> 3% of each run, Pallas kernels for 0% -> 0%
where the time goes in v1:
time: 684 us; the launch traced here: 680 us
  waiting for transfers between devices  551 us (81%)
  blocking collectives  38.8 us (6%)
  starting transfers between devices  28.5 us (4%)
  matrix products  20.5 us (3%)
  between operations  15.7 us (2%)
  other arithmetic  12.7 us (2%)
  local copies, waits for them, and re-layouts  12.5 us (2%)
    all_to_all x1, waiting for transfers between devices, on_device(): lax.all_to_all(jnp.stack([o_weight] * lax.axis_size('dp')), 'dp', 0, 0)  346 us
    all_gather x1, waiting for transfers between devices, in_one_piece(): filled = lax.all_gather(both, axis, axis=dim, tiled=True)  178 us
    all_to_all x1, blocking collectives, deliver(): lax.all_to_all(outgoing, 'dp', split_axis=0, concat_axis=0, tiled=True)  26.7 us
    all_to_all x1, waiting for transfers between devices, deliver(): spread = lax.all_to_all(flat, 'dp', split_axis=0, concat_axis=0, tiled=True)  18.6 us
  transfers between devices with their start and end apart: 4, of which 4 were waited for; matrix products, arithmetic and copies ran while one was open for 3% of the time, Pallas kernels for 0%

profile of v1, /device:TPU:38, one launch (start us, length us, event | category | flops | bytes accessed | tf_op | source)
XLA Modules:
  0.0 679.6 jit_solution(14051960783982347609)
XLA Ops:
  7.3 1.0 copy.79
  8.2 1.6 pad_maximum_fusion.1
  11.2 0.3 multiply_cosine_fusion
  11.5 0.1 copy.59
  11.6 0.1 copy.60
  11.8 177.7 %all-gather.2.cloned.1.call-done = bf16[4096,1536]{1,0:T(8,128)(2,1)} async-done(((bf16[64,1536]{1,0:T(8,128)(2,1)}), bf16[4096,1536]{1,0:T(8,128)(2,1)}) %all-gather.2.cloned.1.call-update) | async-done | bytes 12582928 | tf_op jit(solution)/shard_map/all_gather | solution.py:32
  189.5 3.5 fusion.3
  193.0 0.1 copy.78
  193.1 0.1 copy.77
  193.3 0.2 subtract_convert_fusion.1
  193.5 0.1 fusion.22
  193.6 0.5 copy-done.3
  194.2 0.3 copy.65
  194.5 4.0 all_to_all.50
  198.4 0.6 broadcast_in_dim.76
  199.1 12.5 %all-to-all-start.2 = ((s32[64,1,1]{2,1,0:T(1,128)}), s32[64,1,1]{2,1,0:T(1,128)S(1)}, u32[]{:S(2)}, u32[]{:S(2)}) async-start(s32[64,1,1]{2,1,0:T(1,128)} %broadcast_in_dim.76), calls=%async_computation.2 | async-start | bytes 65536 | tf_op jit(solution)/shard_map/all_to_all | solution.py:13
  211.6 0.1 all_to_all.43
  211.7 0.5 broadcast.135
  212.3 2.1 reduce.2
  214.4 0.9 reshape.182
  215.3 8.1 %all-to-all-done.2 = s32[64,1,1]{2,1,0:T(1,128)S(1)} async-done(((s32[64,1,1]{2,1,0:T(1,128)}), s32[64,1,1]{2,1,0:T(1,128)S(1)}, u32[]{:S(2)}, u32[]{:S(2)}) %all-to-all-start.2) | async-done | bytes 288 | tf_op jit(solution)/shard_map/all_to_all | solution.py:13
  223.4 8.1 %all-to-all-start.4 = ((bf16[64,2,1024]{2,1,0:T(2,128)(2,1)}), bf16[64,2,1024]{2,1,0:T(2,128)(2,1)S(1)}, u32[]{:S(2)}, u32[]{:S(2)}) async-start(bf16[64,2,1024]{2,1,0:T(2,128)(2,1)} %reshape.182), calls=%async_computation.4 | async-start | bytes 524288 | tf_op jit(solution)/shard_map/all_to_all | solution.py:97
  231.5 1.2 reduce
  232.7 0.1 select_reduce_fusion
  232.9 18.6 %all-to-all-done.4 = bf16[64,2,1024]{2,1,0:T(2,128)(2,1)S(1)} async-done(((bf16[64,2,1024]{2,1,0:T(2,128)(2,1)}), bf16[64,2,1024]{2,1,0:T(2,128)(2,1)S(1)}, u32[]{:S(2)}, u32[]{:S(2)}) %all-to-all-start.4) | async-done | bytes 262176 | tf_op jit(solution)/shard_map/all_to_all | solution.py:97
  251.4 0.2 reshape.183
  251.6 0.2 copy.82
  251.8 0.7 gather_fusion
  252.6 0.1 bitcast_select_fusion
  252.7 0.7 reduce.3
  253.4 0.2 reshape.184
  253.6 26.7 %all_to_all.51 = bf16[64,2,1024]{2,1,0:T(2,128)(2,1)S(1)} all-to-all(bf16[64,2,1024]{2,1,0:T(2,128)(2,1)S(1)} %reshape.184), channel_id=1, replica_groups=mesh['parts'=2,'dp'=64,'tensor'=2] {'dp'}, dimensions={0} | all-to-all | bytes 524288 | tf_op jit(solution)/shard_map/all_to_all | solution.py:102
  280.3 4.4 stack.8
  284.6 7.9 %all-to-all-start = ((bf16[64,1024,64]{1,2,0:T(8,128)(2,1)}), bf16[64,1024,64]{1,2,0:T(8,128)(2,1)}, u32[]{:S(2)}, u32[]{:S(2)}) async-start(bf16[64,1024,64]{1,2,0:T(8,128)(2,1)} %stack.8), calls=%async_computation | async-start | bytes 16777216 | tf_op jit(solution)/shard_map/all_to_all | solution.py:130
  292.5 0.7 fusion.14
  293.2 5.8 fusion.1
  299.0 0.2 subtract_convert_fusion
  299.2 0.3 copy.56
  299.5 1.0 copy.57
  300.5 3.5 fusion.30
  304.0 1.9 convolution_convert_fusion
  305.9 0.2 reshape.185
  306.2 1.5 reduce.1
  307.7 0.8 broadcast_in_dim_reshape.4
  308.5 346.5 %all-to-all-done = bf16[64,1024,64]{1,2,0:T(8,128)(2,1)} async-done(((bf16[64,1024,64]{1,2,0:T(8,128)(2,1)}), bf16[64,1024,64]{1,2,0:T(8,128)(2,1)}, u32[]{:S(2)}, u32[]{:S(2)}) %all-to-all-start) | async-done | bytes 8388640 | tf_op jit(solution)/shard_map/all_to_all | solution.py:130
  655.0 5.8 convolution_bitcast_fusion
  660.8 8.2 %all_to_all.52 = f32[2,256,2048]{2,1,0:T(8,128)} all-to-all(f32[2,256,2048]{2,1,0:T(8,128)S(1)} %convolution_bitcast_fusion), channel_id=1, replica_groups=mesh['parts'=2,'dp'=64,'tensor'=2] {'tensor'}, dimensions={0} | all-to-all | bytes 8388608 | tf_op jit(solution)/shard_map/all_to_all | solution.py:46
  669.0 3.8 reduce_sum.31
  (23 shorter events, 0.3 us)
Async XLA Ops:
  7.2 182.3 %copy-start = (bf16[1,256,4096]{2,1,0:T(8,128)(2,1)S(1)}, bf16[1,256,4096]{2,1,0:T(8,128)(2,1)}, u32[]{:S(2)}) copy-start(bf16[1,256,4096]{2,1,0:T(8,128)(2,1)} %param.6) | copy-start | bytes 6291460
  7.2 182.3 %all-gather.2.cloned.1.call-start = ((), (), s32[]{:S(2)}) async-start(), calls=%async_computation.6 | async-start | bytes 12779520 | tf_op jit(solution)/shard_map/all_gather | solution.py:32
  193.1 18.4 %copy-start.1 = (bf16[256,1,2,128]{3,0,2,1:T(8,128)(2,1)}, bf16[256,1,2,128]{3,0,2,1:T(8,128)(2,1)S(1)}, u32[]{:S(2)}) copy-start(bf16[256,1,2,128]{3,0,2,1:T(8,128)(2,1)S(1)} %copy.78) | copy-start | bytes 393220
  193.4 0.6 copy-start.3
  193.4 0.7 copy-start.4
  199.1 24.3 %all-to-all-start.2 = ((s32[64,1,1]{2,1,0:T(1,128)}), s32[64,1,1]{2,1,0:T(1,128)S(1)}, u32[]{:S(2)}, u32[]{:S(2)}) async-start(s32[64,1,1]{2,1,0:T(1,128)} %broadcast_in_dim.76), calls=%async_computation.2 | async-start | bytes 65536 | tf_op jit(solution)/shard_map/all_to_all | solution.py:13
  223.4 28.0 %all-to-all-start.4 = ((bf16[64,2,1024]{2,1,0:T(2,128)(2,1)}), bf16[64,2,1024]{2,1,0:T(2,128)(2,1)S(1)}, u32[]{:S(2)}, u32[]{:S(2)}) async-start(bf16[64,2,1024]{2,1,0:T(2,128)(2,1)} %reshape.182), calls=%async_computation.4 | async-start | bytes 524288 | tf_op jit(solution)/shard_map/all_to_all | solution.py:97
  251.8 28.4 %copy-start.5 = (bf16[1024,64]{0,1:T(8,128)(2,1)S(1)}, bf16[1024,64]{0,1:T(8,128)(2,1)}, u32[]{:S(2)}) copy-start(bf16[1024,64]{0,1:T(8,128)(2,1)} %param.9) | copy-start | bytes 393220
  284.6 370.4 %all-to-all-start = ((bf16[64,1024,64]{1,2,0:T(8,128)(2,1)}), bf16[64,1024,64]{1,2,0:T(8,128)(2,1)}, u32[]{:S(2)}, u32[]{:S(2)}) async-start(bf16[64,1024,64]{1,2,0:T(8,128)(2,1)} %stack.8), calls=%async_computation | async-start | bytes 16777216 | tf_op jit(solution)/shard_map/all_to_all | solution.py:130
  300.5 3.5 copy-start.2
Sparse Core Ops, SparseCore 0:
  11.0 178.4 all-gather.1
